TPU v7x, 32 devices: a whole 2x2x4 slice. The times are simulated.
32 devices in a mesh: curve: 8 (over z, x), level: 4 (over y, core).
Axes of the slice: x: 2, y: 2, z: 4, core: 2. Of those that a mesh axis runs over, the one named last changes fastest.
Arguments:
- right_side: float32 [512, 4096], P(None, ('curve', 'level')), may hold values from -6 to 6
- counts: int32 [32], replicated, may hold values from 96 to 128, as said below
- neighbours: int32 [6, 4096], P(None, ('curve', 'level')), may hold values from -1 to 4095, as said below
Outputs:
- solution: float32 [512, 4096], P(None, ('curve', 'level'))
- residual: float32 [512, 4096], P(None, ('curve', 'level'))
- residual_norm: float32 [], replicated
Inputs may be any that keep to these rules, and one draw needn't show every extreme that they name: `counts`: some device holds 128 live bricks and some device holds 96. `neighbours`: A slot's global number is its device times 128 plus its position. The relation is symmetric across opposite faces; padding slots have -1 on every face and no brick names them. Live bricks are numbered along the curve; the brick across face 0, 2 or 4 lies earlier on the curve and the one across face 1, 3 or 5 later, at most 256 live bricks away.
All inputs are finite; a program needn't handle non-finite values.
Results may differ from a plain program's by a relative error of at most 0.00027.
Values sent between devices are 32-bit elements; how exact they have to be, the bound alone decides.
A program may use at most 64 MiB of HBM per device.

v0:
```python
import jax
import jax.numpy as jnp
from jax import lax
from jax.sharding import PartitionSpec as P

MIN_LIVE = 96
LAYER = 256
HOPS = 3
OPPOSITE = (1, 0, 3, 2, 5, 4)
RELAXATION = 2.0 / 3.0


def from_behind(block, axis, distance):
    devices = range(lax.axis_size(axis))
    route = [(i - distance, i) for i in devices if i - distance in devices]
    return lax.ppermute(block, axis, route)


def brick_faces(values, extent):
    volume = values.reshape(extent, extent, extent, -1)
    surfaces = [
        volume[0],
        volume[extent - 1],
        volume[:, 0],
        volume[:, extent - 1],
        volume[:, :, 0],
        volume[:, :, extent - 1],
    ]
    return jnp.stack([one_face.reshape(extent * extent, -1) for one_face in surfaces])


def apply_operator(values, ghosts, extent, weight):
    brick_count = values.shape[1]
    volume = values.reshape(extent, extent, extent, brick_count)
    padded = jnp.pad(volume, ((1, 1), (1, 1), (1, 1), (0, 0)))
    shaped = [ghost.reshape(extent, extent, brick_count) for ghost in ghosts]
    padded = padded.at[0, 1:-1, 1:-1].set(shaped[0])
    padded = padded.at[-1, 1:-1, 1:-1].set(shaped[1])
    padded = padded.at[1:-1, 0, 1:-1].set(shaped[2])
    padded = padded.at[1:-1, -1, 1:-1].set(shaped[3])
    padded = padded.at[1:-1, 1:-1, 0].set(shaped[4])
    padded = padded.at[1:-1, 1:-1, -1].set(shaped[5])
    beside = padded[2:, 1:-1, 1:-1] + padded[:-2, 1:-1, 1:-1]
    beside = beside + padded[1:-1, 2:, 1:-1] + padded[1:-1, :-2, 1:-1]
    beside = beside + padded[1:-1, 1:-1, 2:] + padded[1:-1, 1:-1, :-2]
    return ((6.0 * volume - beside) * weight).reshape(extent * extent * extent, brick_count)


def restrict(values):
    brick_count = values.shape[1]
    grouped = values.reshape(4, 2, 4, 2, 4, 2, brick_count)
    return jnp.mean(grouped, axis=(1, 3, 5)).reshape(64, brick_count)


def prolong(coarse):
    brick_count = coarse.shape[1]
    spread = jnp.broadcast_to(
        coarse.reshape(4, 1, 4, 1, 4, 1, brick_count), (4, 2, 4, 2, 4, 2, brick_count)
    )
    return spread.reshape(512, brick_count)


def precondition(residual_in, exchange):
    relax_fine = RELAXATION / 6.0
    relax_coarse = RELAXATION / 1.5
    sweep_one = relax_fine * residual_in
    sweep_two = sweep_one + relax_fine * (
        residual_in - apply_operator(sweep_one, exchange(brick_faces(sweep_one, 8)), 8, 1.0)
    )
    defect = residual_in - apply_operator(sweep_two, exchange(brick_faces(sweep_two, 8)), 8, 1.0)
    coarse_rhs = restrict(defect)
    coarse_one = relax_coarse * coarse_rhs
    coarse_two = coarse_one + relax_coarse * (
        coarse_rhs - apply_operator(coarse_one, exchange(brick_faces(coarse_one, 4)), 4, 0.25)
    )
    sweep_three = sweep_two + prolong(coarse_two)
    return sweep_three + relax_fine * (
        residual_in - apply_operator(sweep_three, exchange(brick_faces(sweep_three, 8)), 8, 1.0)
    )


def local(right_side, counts, neighbours):
    slot_count = right_side.shape[1]
    device = lax.axis_index(("curve", "level"))
    own_count = counts[device]
    live_slot = jnp.arange(slot_count, dtype=jnp.int32) < own_count
    residual_in = jnp.where(live_slot[None, :], right_side, jnp.zeros_like(right_side))
    widths = [min(slot_count, LAYER - (hop - 1) * MIN_LIVE) for hop in range(1, HOPS + 1)]
    window_starts = []
    running = slot_count
    for width in widths:
        window_starts.append(running)
        running = running + width
    width_table = jnp.array(widths, dtype=jnp.int32)
    start_table = jnp.array(window_starts, dtype=jnp.int32)
    present = neighbours >= 0
    safe_slot = jnp.where(present, neighbours, 0)
    owner = safe_slot // slot_count
    offset = safe_slot % slot_count
    earlier = (jnp.arange(6, dtype=jnp.int32) % 2 == 0)[:, None]
    hop_index = jnp.clip(jnp.where(earlier, device - owner, owner - device), 1, HOPS) - 1
    skipped = jnp.where(earlier, jnp.maximum(counts[owner] - width_table[hop_index], 0), 0)
    position = jnp.where(owner == device, offset, start_table[hop_index] + offset - skipped)
    position = jnp.clip(jnp.where(present, position, 0), 0, running - 1)

    def exchange(surface):
        odd_faces = surface[1::2]
        even_faces = surface[0::2]
        lower = []
        upper = []
        for hop in range(1, HOPS + 1):
            width = widths[hop - 1]
            piece = lax.dynamic_slice_in_dim(odd_faces, jnp.maximum(own_count - width, 0), width, 2)
            lower.append(from_behind(piece, ("curve", "level"), hop))
            upper.append(from_behind(even_faces[:, :, :width], ("curve", "level"), -hop))
        ghosts = []
        for face_id in range(6):
            windows = lower if face_id % 2 == 0 else upper
            lookup = jnp.concatenate(
                [surface[OPPOSITE[face_id]]] + [window[face_id // 2] for window in windows], axis=1
            )
            picked = jnp.take(lookup, position[face_id], axis=1)
            ghosts.append(jnp.where(present[face_id][None, :], picked, jnp.zeros_like(picked)))
        return ghosts

    preconditioned = precondition(residual_in, exchange)
    image = apply_operator(preconditioned, exchange(brick_faces(preconditioned, 8)), 8, 1.0)
    local_along = jnp.sum(residual_in * preconditioned)
    local_curvature = jnp.sum(preconditioned * image)
    along, curvature, old_square, cross_term, image_square = lax.psum(
        (
            local_along,
            local_curvature,
            jnp.sum(residual_in * residual_in),
            jnp.sum(residual_in * image),
            jnp.sum(image * image),
        ),
        ("curve", "level"),
    )
    step_size = along / curvature
    solution = step_size * preconditioned
    residual = residual_in - step_size * image
    norm_square = old_square - 2.0 * step_size * cross_term + step_size * step_size * image_square
    return (solution, residual, jnp.sqrt(norm_square))


def solution(mesh):
    in_specs = (P(None, ("curve", "level")), P(), P(None, ("curve", "level")))
    out_specs = (P(None, ("curve", "level")), P(None, ("curve", "level")), P())
    return jax.shard_map(local, mesh=mesh, in_specs=in_specs, out_specs=out_specs, check_vma=False)
```

profile of v0, /device:TPU:0, one launch (start us, length us, event | category | flops | bytes accessed | tf_op | source)
XLA Modules:
  0.0 247.6 jit_solution(9839667775032948823)
XLA Ops:
  7.1 6.2 %collective-permute-start.1 = (f32[3,64,128]{1,2,0:T(8,128)S(1)}, f32[3,64,128]{1,2,0:T(8,128)S(1)}, u32[]{:S(2)}, u32[]{:S(2)}) collective-permute-start(f32[3,64,128]{1,2,0:T(8,128)S(1)} %get-tuple-element.404), channel_id=1, source_target_pairs={{0,2},{1,3},{2,4},{3,5},{4,6},{5,7},{6,8},{7,9},{8,10},{9,11},{10,... | collective-permute-start | bytes 294920 | tf_op jit(solution)/shard_map/ppermute | solution.py:16
  13.3 2.1 collective-permute-start
  16.1 5.5 %collective-permute-start.2 = (f32[3,64,64]{1,2,0:T(8,128)S(1)}, f32[3,64,64]{1,2,0:T(8,128)S(1)}, u32[]{:S(2)}, u32[]{:S(2)}) collective-permute-start(f32[3,64,64]{1,2,0:T(8,128)S(1)} %constant_dynamic-slice_fusion.4), channel_id=1, source_target_pairs={{0,3},{1,4},{2,5},{3,6},{4,7},{5,8},{6,9},{7,10},{8,11},{9,12},{10... | collective-permute-start | bytes 147464 | tf_op jit(solution)/shard_map/ppermute | solution.py:16
  23.0 4.8 %gather_fusion.1 = s32[768]{0:T(1024)S(1)} fusion(s32[32]{0:T(128)S(1)} %copy-done, s32[1024]{0:T(1024)S(1)} %get-tuple-element.555), kind=kCustom, calls=%fused_computation.31 | custom fusion | bytes 9216 | tf_op jit(solution)/shard_map/gather | solution.py:102
  28.5 4.8 %gather_fusion.2 = s32[768]{0:T(1024)S(1)} fusion(s32[3]{0:T(128)S(1)} %copy-done.2, s32[1024]{0:T(1024)S(1)} %get-tuple-element.556), kind=kCustom, calls=%fused_computation.32 | custom fusion | bytes 9216 | tf_op jit(solution)/shard_map/gather | solution.py:102
  33.3 4.8 %gather_fusion = s32[768]{0:T(1024)S(1)} fusion(s32[3]{0:T(128)S(1)} %copy-done.1, s32[1024]{0:T(1024)S(1)} %get-tuple-element.556), kind=kCustom, calls=%fused_computation.30 | custom fusion | bytes 9216 | tf_op jit(solution)/shard_map/gather | solution.py:103
  44.1 4.6 %collective-permute-done.5 = f32[3,64,64]{1,2,0:T(8,128)S(1)} collective-permute-done((f32[3,64,64]{1,2,0:T(8,128)S(1)}, f32[3,64,64]{1,2,0:T(8,128)S(1)}, u32[]{:S(2)}, u32[]{:S(2)}) %collective-permute-start.5) | collective-permute-done | bytes 49184 | tf_op jit(solution)/shard_map/ppermute | solution.py:16
  60.4 3.3 %collective-permute-start.8 = (f32[3,64,64]{1,2,0:T(8,128)S(1)}, f32[3,64,64]{1,2,0:T(8,128)S(1)}, u32[]{:S(2)}, u32[]{:S(2)}) collective-permute-start(f32[3,64,64]{1,2,0:T(8,128)S(1)} %constant_dynamic-slice_fusion.3), channel_id=1, source_target_pairs={{0,3},{1,4},{2,5},{3,6},{4,7},{5,8},{6,9},{7,10},{8,11},{9,12},{10... | collective-permute-start | bytes 147464 | tf_op jit(solution)/shard_map/ppermute | solution.py:16
  66.4 5.4 %collective-permute-start.7 = (f32[3,64,128]{1,2,0:T(8,128)S(1)}, f32[3,64,128]{1,2,0:T(8,128)S(1)}, u32[]{:S(2)}, u32[]{:S(2)}) collective-permute-start(f32[3,64,128]{1,2,0:T(8,128)S(1)} %get-tuple-element.402), channel_id=1, source_target_pairs={{0,2},{1,3},{2,4},{3,5},{4,6},{5,7},{6,8},{7,9},{8,10},{9,11},{10,... | collective-permute-start | bytes 294920 | tf_op jit(solution)/shard_map/ppermute | solution.py:16
  71.8 3.3 %collective-permute-start.6 = (f32[3,64,128]{1,2,0:T(8,128)S(1)}, f32[3,64,128]{1,2,0:T(8,128)S(1)}, u32[]{:S(2)}, u32[]{:S(2)}) collective-permute-start(f32[3,64,128]{1,2,0:T(8,128)S(1)} %get-tuple-element.402), channel_id=1, source_target_pairs={{0,1},{1,2},{2,3},{3,4},{4,5},{5,6},{6,7},{7,8},{8,9},{9,10},{10,1... | collective-permute-start | bytes 294920 | tf_op jit(solution)/shard_map/ppermute | solution.py:16
  77.6 6.5 %collective-permute-done.11 = f32[3,64,64]{1,2,0:T(8,128)S(1)} collective-permute-done((f32[3,64,64]{1,2,0:T(8,128)S(1)}, f32[3,64,64]{1,2,0:T(8,128)S(1)}, u32[]{:S(2)}, u32[]{:S(2)}) %collective-permute-start.11) | collective-permute-done | bytes 49184 | tf_op jit(solution)/shard_map/ppermute | solution.py:16
  97.2 3.9 %collective-permute-start.14 = (f32[3,16,64]{2,1,0:T(8,128)S(1)}, f32[3,16,64]{2,1,0:T(8,128)S(1)}, u32[]{:S(2)}, u32[]{:S(2)}) collective-permute-start(f32[3,16,64]{2,1,0:T(8,128)S(1)} %constant_dynamic-slice_fusion.2), channel_id=1, source_target_pairs={{0,3},{1,4},{2,5},{3,6},{4,7},{5,8},{6,9},{7,10},{8,11},{9,12},{10... | collective-permute-start | bytes 36872 | tf_op jit(solution)/shard_map/ppermute | solution.py:16
  103.7 6.0 %collective-permute-start.13 = (f32[3,16,128]{2,1,0:T(8,128)S(1)}, f32[3,16,128]{2,1,0:T(8,128)S(1)}, u32[]{:S(2)}, u32[]{:S(2)}) collective-permute-start(f32[3,16,128]{2,1,0:T(8,128)S(1)} %get-tuple-element.510), channel_id=1, source_target_pairs={{0,2},{1,3},{2,4},{3,5},{4,6},{5,7},{6,8},{7,9},{8,10},{9,11},{10,... | collective-permute-start | bytes 73736 | tf_op jit(solution)/shard_map/ppermute | solution.py:16
  109.7 2.1 collective-permute-start.12
  113.2 5.7 %collective-permute-done.17 = f32[3,16,64]{2,1,0:T(8,128)S(1)} collective-permute-done((f32[3,16,64]{2,1,0:T(8,128)S(1)}, f32[3,16,64]{2,1,0:T(8,128)S(1)}, u32[]{:S(2)}, u32[]{:S(2)}) %collective-permute-start.17) | collective-permute-done | bytes 12320 | tf_op jit(solution)/shard_map/ppermute | solution.py:16
  127.3 3.9 %collective-permute-start.20 = (f32[3,64,64]{1,2,0:T(8,128)S(1)}, f32[3,64,64]{1,2,0:T(8,128)S(1)}, u32[]{:S(2)}, u32[]{:S(2)}) collective-permute-start(f32[3,64,64]{1,2,0:T(8,128)S(1)} %constant_dynamic-slice_fusion.1), channel_id=1, source_target_pairs={{0,3},{1,4},{2,5},{3,6},{4,7},{5,8},{6,9},{7,10},{8,11},{9,12},{10... | collective-permute-start | bytes 147464 | tf_op jit(solution)/shard_map/ppermute | solution.py:16
  133.9 6.2 %collective-permute-start.19 = (f32[3,64,128]{1,2,0:T(8,128)S(1)}, f32[3,64,128]{1,2,0:T(8,128)S(1)}, u32[]{:S(2)}, u32[]{:S(2)}) collective-permute-start(f32[3,64,128]{1,2,0:T(8,128)S(1)} %get-tuple-element.400), channel_id=1, source_target_pairs={{0,2},{1,3},{2,4},{3,5},{4,6},{5,7},{6,8},{7,9},{8,10},{9,11},{10,... | collective-permute-start | bytes 294920 | tf_op jit(solution)/shard_map/ppermute | solution.py:16
  140.1 2.1 collective-permute-start.18
  144.9 5.7 %collective-permute-done.23 = f32[3,64,64]{1,2,0:T(8,128)S(1)} collective-permute-done((f32[3,64,64]{1,2,0:T(8,128)S(1)}, f32[3,64,64]{1,2,0:T(8,128)S(1)}, u32[]{:S(2)}, u32[]{:S(2)}) %collective-permute-start.23) | collective-permute-done | bytes 49184 | tf_op jit(solution)/shard_map/ppermute | solution.py:16
  168.6 5.5 %collective-permute-start.25 = (f32[3,64,128]{1,2,0:T(8,128)S(1)}, f32[3,64,128]{1,2,0:T(8,128)S(1)}, u32[]{:S(2)}, u32[]{:S(2)}) collective-permute-start(f32[3,64,128]{1,2,0:T(8,128)S(1)} %get-tuple-element.398), channel_id=1, source_target_pairs={{0,2},{1,3},{2,4},{3,5},{4,6},{5,7},{6,8},{7,9},{8,10},{9,11},{10,... | collective-permute-start | bytes 294920 | tf_op jit(solution)/shard_map/ppermute | solution.py:16
  174.2 3.0 %collective-permute-start.24 = (f32[3,64,128]{1,2,0:T(8,128)S(1)}, f32[3,64,128]{1,2,0:T(8,128)S(1)}, u32[]{:S(2)}, u32[]{:S(2)}) collective-permute-start(f32[3,64,128]{1,2,0:T(8,128)S(1)} %get-tuple-element.398), channel_id=1, source_target_pairs={{0,1},{1,2},{2,3},{3,4},{4,5},{5,6},{6,7},{7,8},{8,9},{9,10},{10,1... | collective-permute-start | bytes 294920 | tf_op jit(solution)/shard_map/ppermute | solution.py:16
  177.7 5.5 %collective-permute-start.26 = (f32[3,64,64]{1,2,0:T(8,128)}, f32[3,64,64]{1,2,0:T(8,128)S(1)}, u32[]{:S(2)}, u32[]{:S(2)}) collective-permute-start(f32[3,64,64]{1,2,0:T(8,128)} %constant_dynamic-slice_fusion), channel_id=1, source_target_pairs={{0,3},{1,4},{2,5},{3,6},{4,7},{5,8},{6,9},{7,10},{8,11},{9,12},{10... | collective-permute-start | bytes 147464 | tf_op jit(solution)/shard_map/ppermute | solution.py:16
  183.8 1.9 collective-permute-done.26
  198.2 43.2 %all-reduce.5 = (f32[]{:T(128)}, f32[]{:T(128)}, f32[]{:T(128)}, f32[]{:T(128)}, f32[]{:T(128)}) all-reduce(f32[]{:T(128)} %get-tuple-element.375, f32[]{:T(128)} %get-tuple-element.376, f32[]{:T(128)} %get-tuple-element.377, f32[]{:T(128)} %get-tuple-element.374, ...), channel_id=1, replica_groups=mesh['curve'=8,'level'=4] {'curve','level'}, use_global_device_ids=true, to_apply=%region_2.5 | all-reduce | flops 5 | bytes 40 | tf_op jit(solution)/shard_map/psum | solution.py:130
  (484 shorter events, 93.2 us)
Async XLA Ops:
  4.5 44.2 %collective-permute-start.4 = (f32[3,64,128]{1,2,0:T(8,128)S(1)}, f32[3,64,128]{1,2,0:T(8,128)S(1)}, u32[]{:S(2)}, u32[]{:S(2)}) collective-permute-start(f32[3,64,128]{1,2,0:T(8,128)S(1)} %get-tuple-element.403), channel_id=1, source_target_pairs={{2,0},{3,1},{4,2},{5,3},{6,4},{7,5},{8,6},{9,7},{10,8},{11,9},{12,... | collective-permute-start | bytes 294920 | tf_op jit(solution)/shard_map/ppermute | solution.py:16
  5.8 42.9 %collective-permute-start.3 = (f32[3,64,128]{1,2,0:T(8,128)S(1)}, f32[3,64,128]{1,2,0:T(8,128)S(1)}, u32[]{:S(2)}, u32[]{:S(2)}) collective-permute-start(f32[3,64,128]{1,2,0:T(8,128)S(1)} %get-tuple-element.403), channel_id=1, source_target_pairs={{1,0},{2,1},{3,2},{4,3},{5,4},{6,5},{7,6},{8,7},{9,8},{10,9},{11,1... | collective-permute-start | bytes 294920 | tf_op jit(solution)/shard_map/ppermute | solution.py:16
  7.1 45.5 %collective-permute-start.1 = (f32[3,64,128]{1,2,0:T(8,128)S(1)}, f32[3,64,128]{1,2,0:T(8,128)S(1)}, u32[]{:S(2)}, u32[]{:S(2)}) collective-permute-start(f32[3,64,128]{1,2,0:T(8,128)S(1)} %get-tuple-element.404), channel_id=1, source_target_pairs={{0,2},{1,3},{2,4},{3,5},{4,6},{5,7},{6,8},{7,9},{8,10},{9,11},{10,... | collective-permute-start | bytes 294920 | tf_op jit(solution)/shard_map/ppermute | solution.py:16
  13.3 40.3 %collective-permute-start = (f32[3,64,128]{1,2,0:T(8,128)S(1)}, f32[3,64,128]{1,2,0:T(8,128)S(1)}, u32[]{:S(2)}, u32[]{:S(2)}) collective-permute-start(f32[3,64,128]{1,2,0:T(8,128)S(1)} %get-tuple-element.404), channel_id=1, source_target_pairs={{0,1},{1,2},{2,3},{3,4},{4,5},{5,6},{6,7},{7,8},{8,9},{9,10},{10,1... | collective-permute-start | bytes 294920 | tf_op jit(solution)/shard_map/ppermute | solution.py:16
  16.1 26.6 %collective-permute-start.2 = (f32[3,64,64]{1,2,0:T(8,128)S(1)}, f32[3,64,64]{1,2,0:T(8,128)S(1)}, u32[]{:S(2)}, u32[]{:S(2)}) collective-permute-start(f32[3,64,64]{1,2,0:T(8,128)S(1)} %constant_dynamic-slice_fusion.4), channel_id=1, source_target_pairs={{0,3},{1,4},{2,5},{3,6},{4,7},{5,8},{6,9},{7,10},{8,11},{9,12},{10... | collective-permute-start | bytes 147464 | tf_op jit(solution)/shard_map/ppermute | solution.py:16
  60.4 15.2 %collective-permute-start.8 = (f32[3,64,64]{1,2,0:T(8,128)S(1)}, f32[3,64,64]{1,2,0:T(8,128)S(1)}, u32[]{:S(2)}, u32[]{:S(2)}) collective-permute-start(f32[3,64,64]{1,2,0:T(8,128)S(1)} %constant_dynamic-slice_fusion.3), channel_id=1, source_target_pairs={{0,3},{1,4},{2,5},{3,6},{4,7},{5,8},{6,9},{7,10},{8,11},{9,12},{10... | collective-permute-start | bytes 147464 | tf_op jit(solution)/shard_map/ppermute | solution.py:16
  63.8 20.9 %collective-permute-start.10 = (f32[3,64,128]{1,2,0:T(8,128)S(1)}, f32[3,64,128]{1,2,0:T(8,128)S(1)}, u32[]{:S(2)}, u32[]{:S(2)}) collective-permute-start(f32[3,64,128]{1,2,0:T(8,128)S(1)} %get-tuple-element.401), channel_id=1, source_target_pairs={{2,0},{3,1},{4,2},{5,3},{6,4},{7,5},{8,6},{9,7},{10,8},{11,9},{12,... | collective-permute-start | bytes 294920 | tf_op jit(solution)/shard_map/ppermute | solution.py:16
  65.1 19.6 %collective-permute-start.9 = (f32[3,64,128]{1,2,0:T(8,128)S(1)}, f32[3,64,128]{1,2,0:T(8,128)S(1)}, u32[]{:S(2)}, u32[]{:S(2)}) collective-permute-start(f32[3,64,128]{1,2,0:T(8,128)S(1)} %get-tuple-element.401), channel_id=1, source_target_pairs={{1,0},{2,1},{3,2},{4,3},{5,4},{6,5},{7,6},{8,7},{9,8},{10,9},{11,1... | collective-permute-start | bytes 294920 | tf_op jit(solution)/shard_map/ppermute | solution.py:16
  66.4 22.4 %collective-permute-start.7 = (f32[3,64,128]{1,2,0:T(8,128)S(1)}, f32[3,64,128]{1,2,0:T(8,128)S(1)}, u32[]{:S(2)}, u32[]{:S(2)}) collective-permute-start(f32[3,64,128]{1,2,0:T(8,128)S(1)} %get-tuple-element.402), channel_id=1, source_target_pairs={{0,2},{1,3},{2,4},{3,5},{4,6},{5,7},{6,8},{7,9},{8,10},{9,11},{10,... | collective-permute-start | bytes 294920 | tf_op jit(solution)/shard_map/ppermute | solution.py:16
  71.8 18.1 %collective-permute-start.6 = (f32[3,64,128]{1,2,0:T(8,128)S(1)}, f32[3,64,128]{1,2,0:T(8,128)S(1)}, u32[]{:S(2)}, u32[]{:S(2)}) collective-permute-start(f32[3,64,128]{1,2,0:T(8,128)S(1)} %get-tuple-element.402), channel_id=1, source_target_pairs={{0,1},{1,2},{2,3},{3,4},{4,5},{5,6},{6,7},{7,8},{8,9},{9,10},{10,1... | collective-permute-start | bytes 294920 | tf_op jit(solution)/shard_map/ppermute | solution.py:16
  97.2 14.7 %collective-permute-start.14 = (f32[3,16,64]{2,1,0:T(8,128)S(1)}, f32[3,16,64]{2,1,0:T(8,128)S(1)}, u32[]{:S(2)}, u32[]{:S(2)}) collective-permute-start(f32[3,16,64]{2,1,0:T(8,128)S(1)} %constant_dynamic-slice_fusion.2), channel_id=1, source_target_pairs={{0,3},{1,4},{2,5},{3,6},{4,7},{5,8},{6,9},{7,10},{8,11},{9,12},{10... | collective-permute-start | bytes 36872 | tf_op jit(solution)/shard_map/ppermute | solution.py:16
  101.1 20.9 %collective-permute-start.16 = (f32[3,16,128]{2,1,0:T(8,128)S(1)}, f32[3,16,128]{2,1,0:T(8,128)S(1)}, u32[]{:S(2)}, u32[]{:S(2)}) collective-permute-start(f32[3,16,128]{2,1,0:T(8,128)S(1)} %get-tuple-element.509), channel_id=1, source_target_pairs={{2,0},{3,1},{4,2},{5,3},{6,4},{7,5},{8,6},{9,7},{10,8},{11,9},{12,... | collective-permute-start | bytes 73736 | tf_op jit(solution)/shard_map/ppermute | solution.py:16
  102.4 19.8 %collective-permute-start.15 = (f32[3,16,128]{2,1,0:T(8,128)S(1)}, f32[3,16,128]{2,1,0:T(8,128)S(1)}, u32[]{:S(2)}, u32[]{:S(2)}) collective-permute-start(f32[3,16,128]{2,1,0:T(8,128)S(1)} %get-tuple-element.509), channel_id=1, source_target_pairs={{1,0},{2,1},{3,2},{4,3},{5,4},{6,5},{7,6},{8,7},{9,8},{10,9},{11,1... | collective-permute-start | bytes 73736 | tf_op jit(solution)/shard_map/ppermute | solution.py:16
  103.7 15.2 %collective-permute-start.13 = (f32[3,16,128]{2,1,0:T(8,128)S(1)}, f32[3,16,128]{2,1,0:T(8,128)S(1)}, u32[]{:S(2)}, u32[]{:S(2)}) collective-permute-start(f32[3,16,128]{2,1,0:T(8,128)S(1)} %get-tuple-element.510), channel_id=1, source_target_pairs={{0,2},{1,3},{2,4},{3,5},{4,6},{5,7},{6,8},{7,9},{8,10},{9,11},{10,... | collective-permute-start | bytes 73736 | tf_op jit(solution)/shard_map/ppermute | solution.py:16
  127.3 15.5 %collective-permute-start.20 = (f32[3,64,64]{1,2,0:T(8,128)S(1)}, f32[3,64,64]{1,2,0:T(8,128)S(1)}, u32[]{:S(2)}, u32[]{:S(2)}) collective-permute-start(f32[3,64,64]{1,2,0:T(8,128)S(1)} %constant_dynamic-slice_fusion.1), channel_id=1, source_target_pairs={{0,3},{1,4},{2,5},{3,6},{4,7},{5,8},{6,9},{7,10},{8,11},{9,12},{10... | collective-permute-start | bytes 147464 | tf_op jit(solution)/shard_map/ppermute | solution.py:16
  131.3 19.8 %collective-permute-start.22 = (f32[3,64,128]{1,2,0:T(8,128)S(1)}, f32[3,64,128]{1,2,0:T(8,128)S(1)}, u32[]{:S(2)}, u32[]{:S(2)}) collective-permute-start(f32[3,64,128]{1,2,0:T(8,128)S(1)} %get-tuple-element.399), channel_id=1, source_target_pairs={{2,0},{3,1},{4,2},{5,3},{6,4},{7,5},{8,6},{9,7},{10,8},{11,9},{12,... | collective-permute-start | bytes 294920 | tf_op jit(solution)/shard_map/ppermute | solution.py:16
  132.6 18.6 %collective-permute-start.21 = (f32[3,64,128]{1,2,0:T(8,128)S(1)}, f32[3,64,128]{1,2,0:T(8,128)S(1)}, u32[]{:S(2)}, u32[]{:S(2)}) collective-permute-start(f32[3,64,128]{1,2,0:T(8,128)S(1)} %get-tuple-element.399), channel_id=1, source_target_pairs={{1,0},{2,1},{3,2},{4,3},{5,4},{6,5},{7,6},{8,7},{9,8},{10,9},{11,1... | collective-permute-start | bytes 294920 | tf_op jit(solution)/shard_map/ppermute | solution.py:16
  133.9 21.4 %collective-permute-start.19 = (f32[3,64,128]{1,2,0:T(8,128)S(1)}, f32[3,64,128]{1,2,0:T(8,128)S(1)}, u32[]{:S(2)}, u32[]{:S(2)}) collective-permute-start(f32[3,64,128]{1,2,0:T(8,128)S(1)} %get-tuple-element.400), channel_id=1, source_target_pairs={{0,2},{1,3},{2,4},{3,5},{4,6},{5,7},{6,8},{7,9},{8,10},{9,11},{10,... | collective-permute-start | bytes 294920 | tf_op jit(solution)/shard_map/ppermute | solution.py:16
  140.1 16.2 %collective-permute-start.18 = (f32[3,64,128]{1,2,0:T(8,128)S(1)}, f32[3,64,128]{1,2,0:T(8,128)S(1)}, u32[]{:S(2)}, u32[]{:S(2)}) collective-permute-start(f32[3,64,128]{1,2,0:T(8,128)S(1)} %get-tuple-element.400), channel_id=1, source_target_pairs={{0,1},{1,2},{2,3},{3,4},{4,5},{5,6},{6,7},{7,8},{8,9},{9,10},{10,1... | collective-permute-start | bytes 294920 | tf_op jit(solution)/shard_map/ppermute | solution.py:16
  164.1 22.2 %collective-permute-start.28 = (f32[3,64,128]{1,2,0:T(8,128)S(1)}, f32[3,64,128]{1,2,0:T(8,128)S(1)}, u32[]{:S(2)}, u32[]{:S(2)}) collective-permute-start(f32[3,64,128]{1,2,0:T(8,128)S(1)} %get-tuple-element.397), channel_id=1, source_target_pairs={{2,0},{3,1},{4,2},{5,3},{6,4},{7,5},{8,6},{9,7},{10,8},{11,9},{12,... | collective-permute-start | bytes 294920 | tf_op jit(solution)/shard_map/ppermute | solution.py:16
  165.4 20.9 %collective-permute-start.27 = (f32[3,64,128]{1,2,0:T(8,128)S(1)}, f32[3,64,128]{1,2,0:T(8,128)S(1)}, u32[]{:S(2)}, u32[]{:S(2)}) collective-permute-start(f32[3,64,128]{1,2,0:T(8,128)S(1)} %get-tuple-element.397), channel_id=1, source_target_pairs={{1,0},{2,1},{3,2},{4,3},{5,4},{6,5},{7,6},{8,7},{9,8},{10,9},{11,1... | collective-permute-start | bytes 294920 | tf_op jit(solution)/shard_map/ppermute | solution.py:16
  166.7 11.0 %collective-permute-start.29 = (f32[3,64,64]{1,2,0:T(8,128)S(1)}, f32[3,64,64]{1,2,0:T(8,128)S(1)}, u32[]{:S(2)}, u32[]{:S(2)}) collective-permute-start(f32[3,64,64]{1,2,0:T(8,128)S(1)} %slice.1959), channel_id=1, source_target_pairs={{3,0},{4,1},{5,2},{6,3},{7,4},{8,5},{9,6},{10,7},{11,8},{12,9},{13... | collective-permute-start | bytes 147464 | tf_op jit(solution)/shard_map/ppermute | solution.py:16
  168.6 21.8 %collective-permute-start.25 = (f32[3,64,128]{1,2,0:T(8,128)S(1)}, f32[3,64,128]{1,2,0:T(8,128)S(1)}, u32[]{:S(2)}, u32[]{:S(2)}) collective-permute-start(f32[3,64,128]{1,2,0:T(8,128)S(1)} %get-tuple-element.398), channel_id=1, source_target_pairs={{0,2},{1,3},{2,4},{3,5},{4,6},{5,7},{6,8},{7,9},{8,10},{9,11},{10,... | collective-permute-start | bytes 294920 | tf_op jit(solution)/shard_map/ppermute | solution.py:16
  174.2 17.3 %collective-permute-start.24 = (f32[3,64,128]{1,2,0:T(8,128)S(1)}, f32[3,64,128]{1,2,0:T(8,128)S(1)}, u32[]{:S(2)}, u32[]{:S(2)}) collective-permute-start(f32[3,64,128]{1,2,0:T(8,128)S(1)} %get-tuple-element.398), channel_id=1, source_target_pairs={{0,1},{1,2},{2,3},{3,4},{4,5},{5,6},{6,7},{7,8},{8,9},{9,10},{10,1... | collective-permute-start | bytes 294920 | tf_op jit(solution)/shard_map/ppermute | solution.py:16
  (66 other events, 161.9 us)
where the time goes:
time: 250 us; the launch traced here: 248 us
  starting transfers between devices  83.7 us (33%)
  local copies, waits for them, and re-layouts  76.8 us (31%)
  blocking collectives  43.2 us (17%)
  waiting for transfers between devices  24.4 us (10%)
  other arithmetic  11.1 us (4%)
  between operations  8.26 us (3%)
    ppermute x30, starting transfers between devices, from_behind(): return lax.ppermute(block, axis, route)  83.7 us
    psum x1, blocking collectives, local(): lax.psum((local_along, local_curvature, jnp.sum(residual_in * residual_in...  43.2 us
    ppermute x30, waiting for transfers between devices, from_behind(): return lax.ppermute(block, axis, route)  24.4 us
    gather x30, local copies, waits for them, and re-layouts, exchange(): picked = jnp.take(lookup, position[face_id], axis=1)  23.5 us
    unnamed x148, local copies, waits for them, and re-layouts  20.8 us
  transfers between devices with their start and end apart: 30, of which 5 were waited for; matrix products, arithmetic and copies ran while one was open for 17% of the time, Pallas kernels for 0%

commit v1 on v0

--- a/solution.py
+++ b/solution.py
@@ -127,7 +127,11 @@
     image = apply_operator(preconditioned, exchange(brick_faces(preconditioned, 8)), 8, 1.0)
     local_along = jnp.sum(residual_in * preconditioned)
     local_curvature = jnp.sum(preconditioned * image)
-    along, curvature, old_square, cross_term, image_square = lax.psum(
+
+    def block_balance(matrix, net_axis, along_axis):
+        return lax.psum(lax.psum(matrix, net_axis), along_axis)
+
+    along, curvature, old_square, cross_term, image_square = block_balance(
         (
             local_along,
             local_curvature,
@@ -135,7 +139,8 @@
             jnp.sum(residual_in * image),
             jnp.sum(image * image),
         ),
-        ("curve", "level"),
+        "curve",
+        "level",
     )
     step_size = along / curvature
     solution = step_size * preconditioned

time: 250 us -> 236 us (0.944)
  blocking collectives: 43.2 us -> 29.1 us
    psum x1 -> x2, blocking collectives: 43.2 us -> 29.1 us  [block_balance(): return lax.psum(lax.psum(matrix, net_axis), along_axis)]
  transfers between devices with their start and end apart: 30 -> 30, of which waited for: 5 -> 5; matrix products, arithmetic and copies ran while one was open for 17% -> 18% of each run, Pallas kernels for 0% -> 0%
where the time goes in v1:
time: 236 us; the launch traced here: 234 us
  starting transfers between devices  83.7 us (35%)
  local copies, waits for them, and re-layouts  77.1 us (33%)
  blocking collectives  29.1 us (12%)
  waiting for transfers between devices  24.5 us (10%)
  other arithmetic  11.2 us (5%)
  between operations  8.32 us (4%)
    ppermute x30, starting transfers between devices, from_behind(): return lax.ppermute(block, axis, route)  83.7 us
    psum x2, blocking collectives, block_balance(): return lax.psum(lax.psum(matrix, net_axis), along_axis)  29.1 us
    ppermute x30, waiting for transfers between devices, from_behind(): return lax.ppermute(block, axis, route)  24.5 us
    gather x30, local copies, waits for them, and re-layouts, exchange(): picked = jnp.take(lookup, position[face_id], axis=1)  23.5 us
    unnamed x148, local copies, waits for them, and re-layouts  21.1 us
    gather x1, local copies, waits for them, and re-layouts, local(): counts[owner] - width_table[hop_index]  4.79 us
    gather x1, local copies, waits for them, and re-layouts, local(): start_table[hop_index] + offset - skipped  4.79 us
    gather x1, local copies, waits for them, and re-layouts, local(): width_table[hop_index]  4.78 us
  transfers between devices with their start and end apart: 30, of which 5 were waited for; matrix products, arithmetic and copies ran while one was open for 18% of the time, Pallas kernels for 0%

profile of v1, /device:TPU:0, one launch (start us, length us, event | category | flops | bytes accessed | tf_op | source)
XLA Modules:
  0.0 233.8 jit_solution(12254014277037834243)
XLA Ops:
  7.1 6.2 %collective-permute-start.1 = (f32[3,64,128]{1,2,0:T(8,128)S(1)}, f32[3,64,128]{1,2,0:T(8,128)S(1)}, u32[]{:S(2)}, u32[]{:S(2)}) collective-permute-start(f32[3,64,128]{1,2,0:T(8,128)S(1)} %get-tuple-element.409), channel_id=1, source_target_pairs={{0,2},{1,3},{2,4},{3,5},{4,6},{5,7},{6,8},{7,9},{8,10},{9,11},{10,... | collective-permute-start | bytes 294920 | tf_op jit(solution)/shard_map/ppermute | solution.py:16
  13.3 2.1 collective-permute-start
  16.1 5.5 %collective-permute-start.2 = (f32[3,64,64]{1,2,0:T(8,128)S(1)}, f32[3,64,64]{1,2,0:T(8,128)S(1)}, u32[]{:S(2)}, u32[]{:S(2)}) collective-permute-start(f32[3,64,64]{1,2,0:T(8,128)S(1)} %constant_dynamic-slice_fusion.4), channel_id=1, source_target_pairs={{0,3},{1,4},{2,5},{3,6},{4,7},{5,8},{6,9},{7,10},{8,11},{9,12},{10... | collective-permute-start | bytes 147464 | tf_op jit(solution)/shard_map/ppermute | solution.py:16
  23.0 4.8 %gather_fusion.1 = s32[768]{0:T(1024)S(1)} fusion(s32[32]{0:T(128)S(1)} %copy-done, s32[1024]{0:T(1024)S(1)} %get-tuple-element.560), kind=kCustom, calls=%fused_computation.31 | custom fusion | bytes 9216 | tf_op jit(solution)/shard_map/gather | solution.py:102
  28.5 4.8 %gather_fusion.2 = s32[768]{0:T(1024)S(1)} fusion(s32[3]{0:T(128)S(1)} %copy-done.2, s32[1024]{0:T(1024)S(1)} %get-tuple-element.561), kind=kCustom, calls=%fused_computation.32 | custom fusion | bytes 9216 | tf_op jit(solution)/shard_map/gather | solution.py:102
  33.3 4.8 %gather_fusion = s32[768]{0:T(1024)S(1)} fusion(s32[3]{0:T(128)S(1)} %copy-done.1, s32[1024]{0:T(1024)S(1)} %get-tuple-element.561), kind=kCustom, calls=%fused_computation.30 | custom fusion | bytes 9216 | tf_op jit(solution)/shard_map/gather | solution.py:103
  44.1 4.6 %collective-permute-done.5 = f32[3,64,64]{1,2,0:T(8,128)S(1)} collective-permute-done((f32[3,64,64]{1,2,0:T(8,128)S(1)}, f32[3,64,64]{1,2,0:T(8,128)S(1)}, u32[]{:S(2)}, u32[]{:S(2)}) %collective-permute-start.5) | collective-permute-done | bytes 49184 | tf_op jit(solution)/shard_map/ppermute | solution.py:16
  60.6 3.3 %collective-permute-start.8 = (f32[3,64,64]{1,2,0:T(8,128)S(1)}, f32[3,64,64]{1,2,0:T(8,128)S(1)}, u32[]{:S(2)}, u32[]{:S(2)}) collective-permute-start(f32[3,64,64]{1,2,0:T(8,128)S(1)} %constant_dynamic-slice_fusion.3), channel_id=1, source_target_pairs={{0,3},{1,4},{2,5},{3,6},{4,7},{5,8},{6,9},{7,10},{8,11},{9,12},{10... | collective-permute-start | bytes 147464 | tf_op jit(solution)/shard_map/ppermute | solution.py:16
  66.6 5.4 %collective-permute-start.7 = (f32[3,64,128]{1,2,0:T(8,128)S(1)}, f32[3,64,128]{1,2,0:T(8,128)S(1)}, u32[]{:S(2)}, u32[]{:S(2)}) collective-permute-start(f32[3,64,128]{1,2,0:T(8,128)S(1)} %get-tuple-element.407), channel_id=1, source_target_pairs={{0,2},{1,3},{2,4},{3,5},{4,6},{5,7},{6,8},{7,9},{8,10},{9,11},{10,... | collective-permute-start | bytes 294920 | tf_op jit(solution)/shard_map/ppermute | solution.py:16
  72.1 3.3 %collective-permute-start.6 = (f32[3,64,128]{1,2,0:T(8,128)S(1)}, f32[3,64,128]{1,2,0:T(8,128)S(1)}, u32[]{:S(2)}, u32[]{:S(2)}) collective-permute-start(f32[3,64,128]{1,2,0:T(8,128)S(1)} %get-tuple-element.407), channel_id=1, source_target_pairs={{0,1},{1,2},{2,3},{3,4},{4,5},{5,6},{6,7},{7,8},{8,9},{9,10},{10,1... | collective-permute-start | bytes 294920 | tf_op jit(solution)/shard_map/ppermute | solution.py:16
  77.8 6.5 %collective-permute-done.11 = f32[3,64,64]{1,2,0:T(8,128)S(1)} collective-permute-done((f32[3,64,64]{1,2,0:T(8,128)S(1)}, f32[3,64,64]{1,2,0:T(8,128)S(1)}, u32[]{:S(2)}, u32[]{:S(2)}) %collective-permute-start.11) | collective-permute-done | bytes 49184 | tf_op jit(solution)/shard_map/ppermute | solution.py:16
  97.4 3.9 %collective-permute-start.14 = (f32[3,16,64]{2,1,0:T(8,128)S(1)}, f32[3,16,64]{2,1,0:T(8,128)S(1)}, u32[]{:S(2)}, u32[]{:S(2)}) collective-permute-start(f32[3,16,64]{2,1,0:T(8,128)S(1)} %constant_dynamic-slice_fusion.2), channel_id=1, source_target_pairs={{0,3},{1,4},{2,5},{3,6},{4,7},{5,8},{6,9},{7,10},{8,11},{9,12},{10... | collective-permute-start | bytes 36872 | tf_op jit(solution)/shard_map/ppermute | solution.py:16
  104.0 6.0 %collective-permute-start.13 = (f32[3,16,128]{2,1,0:T(8,128)S(1)}, f32[3,16,128]{2,1,0:T(8,128)S(1)}, u32[]{:S(2)}, u32[]{:S(2)}) collective-permute-start(f32[3,16,128]{2,1,0:T(8,128)S(1)} %get-tuple-element.515), channel_id=1, source_target_pairs={{0,2},{1,3},{2,4},{3,5},{4,6},{5,7},{6,8},{7,9},{8,10},{9,11},{10,... | collective-permute-start | bytes 73736 | tf_op jit(solution)/shard_map/ppermute | solution.py:16
  110.0 2.1 collective-permute-start.12
  113.4 5.7 %collective-permute-done.17 = f32[3,16,64]{2,1,0:T(8,128)S(1)} collective-permute-done((f32[3,16,64]{2,1,0:T(8,128)S(1)}, f32[3,16,64]{2,1,0:T(8,128)S(1)}, u32[]{:S(2)}, u32[]{:S(2)}) %collective-permute-start.17) | collective-permute-done | bytes 12320 | tf_op jit(solution)/shard_map/ppermute | solution.py:16
  127.5 3.9 %collective-permute-start.20 = (f32[3,64,64]{1,2,0:T(8,128)S(1)}, f32[3,64,64]{1,2,0:T(8,128)S(1)}, u32[]{:S(2)}, u32[]{:S(2)}) collective-permute-start(f32[3,64,64]{1,2,0:T(8,128)S(1)} %constant_dynamic-slice_fusion.1), channel_id=1, source_target_pairs={{0,3},{1,4},{2,5},{3,6},{4,7},{5,8},{6,9},{7,10},{8,11},{9,12},{10... | collective-permute-start | bytes 147464 | tf_op jit(solution)/shard_map/ppermute | solution.py:16
  134.2 6.2 %collective-permute-start.19 = (f32[3,64,128]{1,2,0:T(8,128)S(1)}, f32[3,64,128]{1,2,0:T(8,128)S(1)}, u32[]{:S(2)}, u32[]{:S(2)}) collective-permute-start(f32[3,64,128]{1,2,0:T(8,128)S(1)} %get-tuple-element.405), channel_id=1, source_target_pairs={{0,2},{1,3},{2,4},{3,5},{4,6},{5,7},{6,8},{7,9},{8,10},{9,11},{10,... | collective-permute-start | bytes 294920 | tf_op jit(solution)/shard_map/ppermute | solution.py:16
  140.4 2.1 collective-permute-start.18
  145.1 5.7 %collective-permute-done.23 = f32[3,64,64]{1,2,0:T(8,128)S(1)} collective-permute-done((f32[3,64,64]{1,2,0:T(8,128)S(1)}, f32[3,64,64]{1,2,0:T(8,128)S(1)}, u32[]{:S(2)}, u32[]{:S(2)}) %collective-permute-start.23) | collective-permute-done | bytes 49184 | tf_op jit(solution)/shard_map/ppermute | solution.py:16
  168.9 5.5 %collective-permute-start.25 = (f32[3,64,128]{1,2,0:T(8,128)S(1)}, f32[3,64,128]{1,2,0:T(8,128)S(1)}, u32[]{:S(2)}, u32[]{:S(2)}) collective-permute-start(f32[3,64,128]{1,2,0:T(8,128)S(1)} %get-tuple-element.403), channel_id=1, source_target_pairs={{0,2},{1,3},{2,4},{3,5},{4,6},{5,7},{6,8},{7,9},{8,10},{9,11},{10,... | collective-permute-start | bytes 294920 | tf_op jit(solution)/shard_map/ppermute | solution.py:16
  174.5 3.0 %collective-permute-start.24 = (f32[3,64,128]{1,2,0:T(8,128)S(1)}, f32[3,64,128]{1,2,0:T(8,128)S(1)}, u32[]{:S(2)}, u32[]{:S(2)}) collective-permute-start(f32[3,64,128]{1,2,0:T(8,128)S(1)} %get-tuple-element.403), channel_id=1, source_target_pairs={{0,1},{1,2},{2,3},{3,4},{4,5},{5,6},{6,7},{7,8},{8,9},{9,10},{10,1... | collective-permute-start | bytes 294920 | tf_op jit(solution)/shard_map/ppermute | solution.py:16
  177.9 5.5 %collective-permute-start.26 = (f32[3,64,64]{1,2,0:T(8,128)}, f32[3,64,64]{1,2,0:T(8,128)S(1)}, u32[]{:S(2)}, u32[]{:S(2)}) collective-permute-start(f32[3,64,64]{1,2,0:T(8,128)} %constant_dynamic-slice_fusion), channel_id=1, source_target_pairs={{0,3},{1,4},{2,5},{3,6},{4,7},{5,8},{6,9},{7,10},{8,11},{9,12},{10... | collective-permute-start | bytes 147464 | tf_op jit(solution)/shard_map/ppermute | solution.py:16
  198.5 22.4 %all-reduce.5 = (f32[]{:T(128)}, f32[]{:T(128)}, f32[]{:T(128)}, f32[]{:T(128)}, f32[]{:T(128)}) all-reduce(f32[]{:T(128)} %get-tuple-element.375, f32[]{:T(128)} %get-tuple-element.376, f32[]{:T(128)} %get-tuple-element.377, f32[]{:T(128)} %get-tuple-element.374, f32[]{:T(128)} %get-tuple-element.388), channel_id=1, replica_groups=mesh['curve'=8,'level'=4] {'curve'}, use_global_device_ids=true, to_apply=%region_2.5 | all-reduce | flops 5 | bytes 40 | tf_op jit(solution)/shard_map/psum | solution.py:132
  220.9 6.7 %all-reduce.6 = (f32[]{:T(128)}, f32[]{:T(128)}, f32[]{:T(128)}, f32[]{:T(128)}, f32[]{:T(128)}) all-reduce(f32[]{:T(128)} %get-tuple-element.378, f32[]{:T(128)} %get-tuple-element.379, f32[]{:T(128)} %get-tuple-element.380, f32[]{:T(128)} %get-tuple-element.381, f32[]{:T(128)} %get-tuple-element.382), channel_id=1, replica_groups=mesh['curve'=8,'level'=4] {'level'}, use_global_device_ids=true, to_apply=%region_3.6 | all-reduce | flops 5 | bytes 40 | tf_op jit(solution)/shard_map/psum | solution.py:132
  (485 shorter events, 95.4 us)
Async XLA Ops:
  4.5 44.2 %collective-permute-start.4 = (f32[3,64,128]{1,2,0:T(8,128)S(1)}, f32[3,64,128]{1,2,0:T(8,128)S(1)}, u32[]{:S(2)}, u32[]{:S(2)}) collective-permute-start(f32[3,64,128]{1,2,0:T(8,128)S(1)} %get-tuple-element.408), channel_id=1, source_target_pairs={{2,0},{3,1},{4,2},{5,3},{6,4},{7,5},{8,6},{9,7},{10,8},{11,9},{12,... | collective-permute-start | bytes 294920 | tf_op jit(solution)/shard_map/ppermute | solution.py:16
  5.8 43.0 %collective-permute-start.3 = (f32[3,64,128]{1,2,0:T(8,128)S(1)}, f32[3,64,128]{1,2,0:T(8,128)S(1)}, u32[]{:S(2)}, u32[]{:S(2)}) collective-permute-start(f32[3,64,128]{1,2,0:T(8,128)S(1)} %get-tuple-element.408), channel_id=1, source_target_pairs={{1,0},{2,1},{3,2},{4,3},{5,4},{6,5},{7,6},{8,7},{9,8},{10,9},{11,1... | collective-permute-start | bytes 294920 | tf_op jit(solution)/shard_map/ppermute | solution.py:16
  7.1 45.6 %collective-permute-start.1 = (f32[3,64,128]{1,2,0:T(8,128)S(1)}, f32[3,64,128]{1,2,0:T(8,128)S(1)}, u32[]{:S(2)}, u32[]{:S(2)}) collective-permute-start(f32[3,64,128]{1,2,0:T(8,128)S(1)} %get-tuple-element.409), channel_id=1, source_target_pairs={{0,2},{1,3},{2,4},{3,5},{4,6},{5,7},{6,8},{7,9},{8,10},{9,11},{10,... | collective-permute-start | bytes 294920 | tf_op jit(solution)/shard_map/ppermute | solution.py:16
  13.3 40.4 %collective-permute-start = (f32[3,64,128]{1,2,0:T(8,128)S(1)}, f32[3,64,128]{1,2,0:T(8,128)S(1)}, u32[]{:S(2)}, u32[]{:S(2)}) collective-permute-start(f32[3,64,128]{1,2,0:T(8,128)S(1)} %get-tuple-element.409), channel_id=1, source_target_pairs={{0,1},{1,2},{2,3},{3,4},{4,5},{5,6},{6,7},{7,8},{8,9},{9,10},{10,1... | collective-permute-start | bytes 294920 | tf_op jit(solution)/shard_map/ppermute | solution.py:16
  16.1 26.7 %collective-permute-start.2 = (f32[3,64,64]{1,2,0:T(8,128)S(1)}, f32[3,64,64]{1,2,0:T(8,128)S(1)}, u32[]{:S(2)}, u32[]{:S(2)}) collective-permute-start(f32[3,64,64]{1,2,0:T(8,128)S(1)} %constant_dynamic-slice_fusion.4), channel_id=1, source_target_pairs={{0,3},{1,4},{2,5},{3,6},{4,7},{5,8},{6,9},{7,10},{8,11},{9,12},{10... | collective-permute-start | bytes 147464 | tf_op jit(solution)/shard_map/ppermute | solution.py:16
  60.6 15.2 %collective-permute-start.8 = (f32[3,64,64]{1,2,0:T(8,128)S(1)}, f32[3,64,64]{1,2,0:T(8,128)S(1)}, u32[]{:S(2)}, u32[]{:S(2)}) collective-permute-start(f32[3,64,64]{1,2,0:T(8,128)S(1)} %constant_dynamic-slice_fusion.3), channel_id=1, source_target_pairs={{0,3},{1,4},{2,5},{3,6},{4,7},{5,8},{6,9},{7,10},{8,11},{9,12},{10... | collective-permute-start | bytes 147464 | tf_op jit(solution)/shard_map/ppermute | solution.py:16
  64.0 20.9 %collective-permute-start.10 = (f32[3,64,128]{1,2,0:T(8,128)S(1)}, f32[3,64,128]{1,2,0:T(8,128)S(1)}, u32[]{:S(2)}, u32[]{:S(2)}) collective-permute-start(f32[3,64,128]{1,2,0:T(8,128)S(1)} %get-tuple-element.406), channel_id=1, source_target_pairs={{2,0},{3,1},{4,2},{5,3},{6,4},{7,5},{8,6},{9,7},{10,8},{11,9},{12,... | collective-permute-start | bytes 294920 | tf_op jit(solution)/shard_map/ppermute | solution.py:16
  65.3 19.6 %collective-permute-start.9 = (f32[3,64,128]{1,2,0:T(8,128)S(1)}, f32[3,64,128]{1,2,0:T(8,128)S(1)}, u32[]{:S(2)}, u32[]{:S(2)}) collective-permute-start(f32[3,64,128]{1,2,0:T(8,128)S(1)} %get-tuple-element.406), channel_id=1, source_target_pairs={{1,0},{2,1},{3,2},{4,3},{5,4},{6,5},{7,6},{8,7},{9,8},{10,9},{11,1... | collective-permute-start | bytes 294920 | tf_op jit(solution)/shard_map/ppermute | solution.py:16
  66.6 22.4 %collective-permute-start.7 = (f32[3,64,128]{1,2,0:T(8,128)S(1)}, f32[3,64,128]{1,2,0:T(8,128)S(1)}, u32[]{:S(2)}, u32[]{:S(2)}) collective-permute-start(f32[3,64,128]{1,2,0:T(8,128)S(1)} %get-tuple-element.407), channel_id=1, source_target_pairs={{0,2},{1,3},{2,4},{3,5},{4,6},{5,7},{6,8},{7,9},{8,10},{9,11},{10,... | collective-permute-start | bytes 294920 | tf_op jit(solution)/shard_map/ppermute | solution.py:16
  72.1 18.0 %collective-permute-start.6 = (f32[3,64,128]{1,2,0:T(8,128)S(1)}, f32[3,64,128]{1,2,0:T(8,128)S(1)}, u32[]{:S(2)}, u32[]{:S(2)}) collective-permute-start(f32[3,64,128]{1,2,0:T(8,128)S(1)} %get-tuple-element.407), channel_id=1, source_target_pairs={{0,1},{1,2},{2,3},{3,4},{4,5},{5,6},{6,7},{7,8},{8,9},{9,10},{10,1... | collective-permute-start | bytes 294920 | tf_op jit(solution)/shard_map/ppermute | solution.py:16
  97.4 14.7 %collective-permute-start.14 = (f32[3,16,64]{2,1,0:T(8,128)S(1)}, f32[3,16,64]{2,1,0:T(8,128)S(1)}, u32[]{:S(2)}, u32[]{:S(2)}) collective-permute-start(f32[3,16,64]{2,1,0:T(8,128)S(1)} %constant_dynamic-slice_fusion.2), channel_id=1, source_target_pairs={{0,3},{1,4},{2,5},{3,6},{4,7},{5,8},{6,9},{7,10},{8,11},{9,12},{10... | collective-permute-start | bytes 36872 | tf_op jit(solution)/shard_map/ppermute | solution.py:16
  101.4 20.9 %collective-permute-start.16 = (f32[3,16,128]{2,1,0:T(8,128)S(1)}, f32[3,16,128]{2,1,0:T(8,128)S(1)}, u32[]{:S(2)}, u32[]{:S(2)}) collective-permute-start(f32[3,16,128]{2,1,0:T(8,128)S(1)} %get-tuple-element.514), channel_id=1, source_target_pairs={{2,0},{3,1},{4,2},{5,3},{6,4},{7,5},{8,6},{9,7},{10,8},{11,9},{12,... | collective-permute-start | bytes 73736 | tf_op jit(solution)/shard_map/ppermute | solution.py:16
  102.7 19.8 %collective-permute-start.15 = (f32[3,16,128]{2,1,0:T(8,128)S(1)}, f32[3,16,128]{2,1,0:T(8,128)S(1)}, u32[]{:S(2)}, u32[]{:S(2)}) collective-permute-start(f32[3,16,128]{2,1,0:T(8,128)S(1)} %get-tuple-element.514), channel_id=1, source_target_pairs={{1,0},{2,1},{3,2},{4,3},{5,4},{6,5},{7,6},{8,7},{9,8},{10,9},{11,1... | collective-permute-start | bytes 73736 | tf_op jit(solution)/shard_map/ppermute | solution.py:16
  104.0 15.2 %collective-permute-start.13 = (f32[3,16,128]{2,1,0:T(8,128)S(1)}, f32[3,16,128]{2,1,0:T(8,128)S(1)}, u32[]{:S(2)}, u32[]{:S(2)}) collective-permute-start(f32[3,16,128]{2,1,0:T(8,128)S(1)} %get-tuple-element.515), channel_id=1, source_target_pairs={{0,2},{1,3},{2,4},{3,5},{4,6},{5,7},{6,8},{7,9},{8,10},{9,11},{10,... | collective-permute-start | bytes 73736 | tf_op jit(solution)/shard_map/ppermute | solution.py:16
  127.5 15.5 %collective-permute-start.20 = (f32[3,64,64]{1,2,0:T(8,128)S(1)}, f32[3,64,64]{1,2,0:T(8,128)S(1)}, u32[]{:S(2)}, u32[]{:S(2)}) collective-permute-start(f32[3,64,64]{1,2,0:T(8,128)S(1)} %constant_dynamic-slice_fusion.1), channel_id=1, source_target_pairs={{0,3},{1,4},{2,5},{3,6},{4,7},{5,8},{6,9},{7,10},{8,11},{9,12},{10... | collective-permute-start | bytes 147464 | tf_op jit(solution)/shard_map/ppermute | solution.py:16
  131.6 19.8 %collective-permute-start.22 = (f32[3,64,128]{1,2,0:T(8,128)S(1)}, f32[3,64,128]{1,2,0:T(8,128)S(1)}, u32[]{:S(2)}, u32[]{:S(2)}) collective-permute-start(f32[3,64,128]{1,2,0:T(8,128)S(1)} %get-tuple-element.404), channel_id=1, source_target_pairs={{2,0},{3,1},{4,2},{5,3},{6,4},{7,5},{8,6},{9,7},{10,8},{11,9},{12,... | collective-permute-start | bytes 294920 | tf_op jit(solution)/shard_map/ppermute | solution.py:16
  132.9 18.6 %collective-permute-start.21 = (f32[3,64,128]{1,2,0:T(8,128)S(1)}, f32[3,64,128]{1,2,0:T(8,128)S(1)}, u32[]{:S(2)}, u32[]{:S(2)}) collective-permute-start(f32[3,64,128]{1,2,0:T(8,128)S(1)} %get-tuple-element.404), channel_id=1, source_target_pairs={{1,0},{2,1},{3,2},{4,3},{5,4},{6,5},{7,6},{8,7},{9,8},{10,9},{11,1... | collective-permute-start | bytes 294920 | tf_op jit(solution)/shard_map/ppermute | solution.py:16
  134.2 21.4 %collective-permute-start.19 = (f32[3,64,128]{1,2,0:T(8,128)S(1)}, f32[3,64,128]{1,2,0:T(8,128)S(1)}, u32[]{:S(2)}, u32[]{:S(2)}) collective-permute-start(f32[3,64,128]{1,2,0:T(8,128)S(1)} %get-tuple-element.405), channel_id=1, source_target_pairs={{0,2},{1,3},{2,4},{3,5},{4,6},{5,7},{6,8},{7,9},{8,10},{9,11},{10,... | collective-permute-start | bytes 294920 | tf_op jit(solution)/shard_map/ppermute | solution.py:16
  140.4 16.2 %collective-permute-start.18 = (f32[3,64,128]{1,2,0:T(8,128)S(1)}, f32[3,64,128]{1,2,0:T(8,128)S(1)}, u32[]{:S(2)}, u32[]{:S(2)}) collective-permute-start(f32[3,64,128]{1,2,0:T(8,128)S(1)} %get-tuple-element.405), channel_id=1, source_target_pairs={{0,1},{1,2},{2,3},{3,4},{4,5},{5,6},{6,7},{7,8},{8,9},{9,10},{10,1... | collective-permute-start | bytes 294920 | tf_op jit(solution)/shard_map/ppermute | solution.py:16
  164.4 22.2 %collective-permute-start.28 = (f32[3,64,128]{1,2,0:T(8,128)S(1)}, f32[3,64,128]{1,2,0:T(8,128)S(1)}, u32[]{:S(2)}, u32[]{:S(2)}) collective-permute-start(f32[3,64,128]{1,2,0:T(8,128)S(1)} %get-tuple-element.402), channel_id=1, source_target_pairs={{2,0},{3,1},{4,2},{5,3},{6,4},{7,5},{8,6},{9,7},{10,8},{11,9},{12,... | collective-permute-start | bytes 294920 | tf_op jit(solution)/shard_map/ppermute | solution.py:16
  165.7 20.9 %collective-permute-start.27 = (f32[3,64,128]{1,2,0:T(8,128)S(1)}, f32[3,64,128]{1,2,0:T(8,128)S(1)}, u32[]{:S(2)}, u32[]{:S(2)}) collective-permute-start(f32[3,64,128]{1,2,0:T(8,128)S(1)} %get-tuple-element.402), channel_id=1, source_target_pairs={{1,0},{2,1},{3,2},{4,3},{5,4},{6,5},{7,6},{8,7},{9,8},{10,9},{11,1... | collective-permute-start | bytes 294920 | tf_op jit(solution)/shard_map/ppermute | solution.py:16
  167.0 11.0 %collective-permute-start.29 = (f32[3,64,64]{1,2,0:T(8,128)S(1)}, f32[3,64,64]{1,2,0:T(8,128)S(1)}, u32[]{:S(2)}, u32[]{:S(2)}) collective-permute-start(f32[3,64,64]{1,2,0:T(8,128)S(1)} %slice.1959), channel_id=1, source_target_pairs={{3,0},{4,1},{5,2},{6,3},{7,4},{8,5},{9,6},{10,7},{11,8},{12,9},{13... | collective-permute-start | bytes 147464 | tf_op jit(solution)/shard_map/ppermute | solution.py:16
  168.9 21.8 %collective-permute-start.25 = (f32[3,64,128]{1,2,0:T(8,128)S(1)}, f32[3,64,128]{1,2,0:T(8,128)S(1)}, u32[]{:S(2)}, u32[]{:S(2)}) collective-permute-start(f32[3,64,128]{1,2,0:T(8,128)S(1)} %get-tuple-element.403), channel_id=1, source_target_pairs={{0,2},{1,3},{2,4},{3,5},{4,6},{5,7},{6,8},{7,9},{8,10},{9,11},{10,... | collective-permute-start | bytes 294920 | tf_op jit(solution)/shard_map/ppermute | solution.py:16
  174.5 17.2 %collective-permute-start.24 = (f32[3,64,128]{1,2,0:T(8,128)S(1)}, f32[3,64,128]{1,2,0:T(8,128)S(1)}, u32[]{:S(2)}, u32[]{:S(2)}) collective-permute-start(f32[3,64,128]{1,2,0:T(8,128)S(1)} %get-tuple-element.403), channel_id=1, source_target_pairs={{0,1},{1,2},{2,3},{3,4},{4,5},{5,6},{6,7},{7,8},{8,9},{9,10},{10,1... | collective-permute-start | bytes 294920 | tf_op jit(solution)/shard_map/ppermute | solution.py:16
  (66 other events, 162.4 us)
